TPU v7x, 32 devices: a whole 2x2x4 slice. The times are simulated.
32 devices in a mesh: trow: 4 (over y, x), tcol: 4 (over z), dp: 2 (over core).
Axes of the slice: x: 2, y: 2, z: 4, core: 2. Of those that a mesh axis runs over, the one named last changes fastest.
Arguments:
- embeds: bfloat16 [2048, 1024], P('dp'), may hold values from -6 to 6
- frequencies: bfloat16 [1024, 8192], P(None, ('trow', 'tcol')), may hold values from -0.5 to 0.5
- phases: float32 [8192], P(('trow', 'tcol')), may hold values from -3.140625 to 3.140625
- labels: int32 [2048], P('dp'), may hold values from 0 to 999
- weights: float32 [8192, 1000], P(('tcol', 'dp'), 'trow'), may hold values from -6 to 6
Outputs:
- gram_matrix: float32 [8192, 8192], P(('trow', 'dp'), 'tcol')
- new_weights: float32 [8192, 1000], P(('tcol', 'dp'), 'trow')
All inputs are finite; a program needn't handle non-finite values.
Results may differ from a plain program's by a relative error of at most 0.023.
Values may be sent and summed in bfloat16 or wider, within the bound.
No kernel may reach another device: no remote copies, remote signals or barrier semaphores. Data moves between devices by JAX's collectives and lax.ppermute only.
A program may use at most 128 MiB of HBM per device.

v0:
```python
import jax
import jax.numpy as jnp
from jax import lax
from jax.sharding import PartitionSpec as P

C = 1000
ROOT_TWO = 1.4142135623730951
RIDGE = 0.5
STEP_RATE = 0.5


def broadcast(array, axis, root):
    mine = lax.axis_index(axis) == root
    return lax.psum(jnp.where(mine, array, jnp.zeros_like(array)), axis)


def featurize(embeds, frequencies, phases):
    angles = jnp.dot(embeds, frequencies, preferred_element_type=jnp.float32) + phases
    return (ROOT_TWO * jnp.cos(angles)).astype(jnp.bfloat16)


def shards(embeds, frequencies, phases, labels, weights):
    rows_here = embeds.shape[0]
    n_row = lax.axis_size("trow")
    n_dp = lax.axis_size("dp")
    row_idx = lax.axis_index("trow")
    col_idx = lax.axis_index("tcol")
    dp_idx = lax.axis_index("dp")
    total_rows = rows_here * n_dp
    contract = (((0,), (0,)), ((), ()))
    own_part = featurize(embeds, frequencies, phases)
    left_feats = lax.all_gather(own_part, "tcol", axis=1, tiled=True)
    right_feats = broadcast(left_feats, "trow", col_idx)
    tile_width = left_feats.shape[1]
    sub_rows = tile_width // n_dp
    gram_part = lax.psum_scatter(
        (
            lax.dot_general(left_feats, right_feats, contract, preferred_element_type=jnp.float32)
            / total_rows
        ).astype(jnp.bfloat16),
        "dp",
        scatter_dimension=0,
        tiled=True,
    ).astype(jnp.float32)
    global_rows = row_idx * tile_width + dp_idx * sub_rows + jnp.arange(sub_rows, dtype=jnp.int32)
    global_cols = col_idx * tile_width + jnp.arange(tile_width, dtype=jnp.int32)
    gram_rows = gram_part + RIDGE * (global_rows[:, None] == global_cols[None, :]).astype(
        jnp.float32
    )
    class_width = weights.shape[1]
    class_ids = row_idx * class_width + jnp.arange(class_width, dtype=jnp.int32)
    onehot = (labels[:, None] == class_ids[None, :]).astype(jnp.bfloat16)
    label_term = lax.dot_general(
        right_feats, onehot, contract, preferred_element_type=jnp.float32
    ) * (C / total_rows)
    label_rows = lax.psum_scatter(
        label_term.astype(jnp.bfloat16), "dp", scatter_dimension=0, tiled=True
    ).astype(jnp.float32)
    gram_three = gram_rows.astype(jnp.bfloat16).reshape(sub_rows, n_dp, sub_rows)
    block_ids = jnp.arange(n_row, dtype=jnp.int32)
    local_weights = weights.astype(jnp.bfloat16)[None]
    pieces = lax.all_gather(local_weights, ("trow", "dp"), axis=0, tiled=True)
    positions = jnp.arange(pieces.shape[0], dtype=jnp.int32)
    sub_index = positions % n_dp
    owner_index = positions // n_dp
    chosen = jnp.take(gram_three, sub_index, axis=1)
    products = jnp.einsum("rpk,pkc->rpc", chosen, pieces, preferred_element_type=jnp.float32)
    placing = (owner_index[:, None] == block_ids[None, :]).astype(jnp.float32)
    folded = jnp.einsum("rpc,pi->ric", products, placing)
    curv_local = folded.reshape(sub_rows, n_row * class_width)
    diag_block = lax.dynamic_slice_in_dim(gram_rows, dp_idx * sub_rows, sub_rows, 1)
    diag_local = jnp.diagonal(diag_block) * (row_idx == col_idx).astype(jnp.float32)
    row_total = lax.psum(curv_local.astype(jnp.bfloat16), "tcol").astype(jnp.float32)
    received, diag_vals = (
        broadcast(row_total.astype(jnp.bfloat16), "trow", col_idx).astype(row_total.dtype),
        broadcast(diag_local.astype(jnp.bfloat16), "trow", col_idx).astype(diag_local.dtype),
    )
    curv_mine = lax.dynamic_slice_in_dim(received, row_idx * class_width, class_width, 1)
    updated = weights - STEP_RATE * (curv_mine - label_rows) / diag_vals[:, None]
    return (gram_rows, updated)


def solution(mesh):
    return jax.shard_map(
        shards,
        mesh=mesh,
        in_specs=(
            P("dp", None),
            P(None, ("trow", "tcol")),
            P(("trow", "tcol")),
            P("dp"),
            P(("tcol", "dp"), "trow"),
        ),
        out_specs=(P(("trow", "dp"), "tcol"), P(("tcol", "dp"), "trow")),
        check_vma=False,
    )
```

profile of v0, /device:TPU:0, one launch (start us, length us, event | category | flops | bytes accessed | tf_op | source)
XLA Modules:
  0.0 468.6 jit_solution(4243780087989902327)
XLA Ops:
  8.0 0.0 copy-start
  8.0 0.0 all-gather.4.cloned.1.call-start
  8.1 1.5 copy-done
  9.6 9.6 %multiply_convert_fusion.1 = bf16[1024,512]{1,0:T(8,128)(2,1)} fusion(bf16[1024,1024]{1,0:T(8,128)(2,1)S(1)} %copy-done, bf16[1024,512]{1,0:T(8,128)(2,1)} %param.6, f32[512]{0:T(512)} %param.7), kind=kOutput, calls=%fused_computation.19 | convolution fusion | flops 1075314688 | bytes 4196352 | tf_op jit(solution)/shard_map/dot_general | solution.py:18
  19.2 0.0 all-gather.4.cloned.1.call-update
  19.2 0.0 all-reduce.4.cloned.1.call-start
  19.3 83.6 %all-gather.4.cloned.1.call-done = bf16[1024,2048]{1,0:T(8,128)(2,1)} async-done(((bf16[1024,512]{1,0:T(8,128)(2,1)}), bf16[1024,2048]{1,0:T(8,128)(2,1)}) %all-gather.4.cloned.1.call-update) | async-done | bytes 4194320 | tf_op jit(solution)/shard_map/all_gather | solution.py:32
  102.8 4.5 broadcast_select_fusion
  107.3 0.0 all-reduce.4.cloned.1.call-update
  107.3 0.0 reduce-scatter.3.cloned.1.call-start
  107.4 102.1 %all-reduce.4.cloned.1.call-done = bf16[1024,2048]{1,0:T(8,128)(2,1)} async-done(((bf16[1024,2048]{1,0:T(8,128)(2,1)}), bf16[1024,2048]{1,0:T(8,128)(2,1)}) %all-reduce.4.cloned.1.call-update) | async-done | bytes 4194320 | tf_op jit(solution)/shard_map/psum | solution.py:14
  209.5 14.0 %multiply_convert_fusion = bf16[2048,2048]{1,0:T(8,128)(2,1)} fusion(bf16[1024,2048]{1,0:T(8,128)(2,1)} %all-gather.4.cloned.1.call-done, bf16[1024,2048]{1,0:T(8,128)(2,1)} %all-reduce.4.cloned.1.call-done), kind=kOutput, calls=%fused_computation.7 | convolution fusion | flops 8598323200 | bytes 16777216 | tf_op jit(solution)/shard_map/dot_general | solution.py:38
  223.5 0.0 copy-start.2
  223.5 0.0 reduce-scatter.3.cloned.1.call-update
  223.5 0.0 all-gather.6.cloned.1.call-start
  223.5 1.1 copy-done.2
  224.7 0.8 convert_element_type.51
  225.5 0.0 all-gather.6.cloned.1.call-update
  225.6 0.2 all-reduce.6.cloned.1.call-start
  225.9 14.2 %reduce-scatter.3.cloned.1.call-done = bf16[1024,2048]{1,0:T(8,128)(2,1)} async-done(((bf16[2048,2048]{1,0:T(8,128)(2,1)}), bf16[1024,2048]{1,0:T(8,128)(2,1)}) %reduce-scatter.3.cloned.1.call-update) | async-done | bytes 4194320 | tf_op jit(solution)/shard_map/reduce_scatter | solution.py:36
  240.0 5.8 %fusion.21 = (bf16[1024,2048]{1,0:T(8,128)(2,1)S(1)}, f32[1024,2048]{1,0:T(8,128)}) fusion(s32[2048]{0:T(1024)S(1)} %iota_add_fusion, s32[1024]{0:T(1024)S(1)} %iota_add_fusion.1, bf16[1024,2048]{1,0:T(8,128)(2,1)} %reduce-scatter.3.cloned.1.call-done), kind=kLoop, calls=%fused_computation.49 | loop fusion | flops 10485760 | bytes 16789504 | tf_op jit(solution)/shard_map/convert_element_type | solution.py:59
  245.8 0.6 fusion.22
  246.4 0.2 copy.24
  246.6 1.6 copy.25
  248.1 4.4 gather_fusion.2
  252.5 6.1 %gather_fusion.1 = bf16[8,512,1024]{2,1,0:T(8,128)(2,1)} fusion(bf16[512,2,1024]{2,0,1:T(8,128)(2,1)} %bitcast.32, s32[1024]{0:T(1024)S(1)} %pad_clamp_fusion), kind=kCustom, calls=%fused_computation.1 | custom fusion | bytes 16777248 | tf_op jit(solution)/shard_map/jit(_take)/gather | solution.py:66
  258.6 4.3 all-gather.6.cloned.1.call-done
  262.9 10.8 %fusion = bf16[8,1024,250]{1,2,0:T(8,128)(2,1)} fusion(bf16[8,1024,250]{2,1,0:T(8,128)(2,1)} %bitcast.37, bf16[512,8,1024]{2,0,1:T(8,128)(2,1)} %bitcast.33, bf16[512,8,1024]{2,0,1:T(8,128)(2,1)} %bitcast.34, pred[8]{0:T(512)(128)(4,1)S(1)} %compare_and_fusion), kind=kOutput, calls=%fused_computation.4 | convolution fusion | flops 4236247040 | bytes 24969224 | tf_op jit(solution)/shard_map/rpk,pkc->rpc/dot_general | solution.py:67
  273.8 6.2 %convert_bitcast_fusion = bf16[1024,4,250]{0,1,2:T(4,128)(2,1)} fusion(bf16[8,1024,250]{1,2,0:T(8,128)(2,1)} %fusion, s32[8]{0:T(128)S(1)} %and_select_fusion.2), kind=kOutput, calls=%fused_computation.21 | convolution fusion | flops 16384032 | bytes 6144032 | tf_op jit(solution)/shard_map/rpc,pi->ric/dot_general | solution.py:69
  280.0 0.0 copy-start.3
  280.0 5.1 %copy.12 = bf16[1024,4,250]{2,1,0:T(4,128)(2,1)S(1)} copy(bf16[1024,4,250]{0,1,2:T(4,128)(2,1)} %convert_bitcast_fusion) | data formatting | bytes 4096000 | tf_op jit(solution)/shard_map/convert_element_type | solution.py:73
  285.1 3.0 reshape.100
  288.0 0.0 all-reduce.6.cloned.1.call-update
  288.1 0.0 reduce-scatter.5.cloned.1.call-start
  288.1 0.0 copy-done.3
  288.1 4.7 fusion.8
  292.8 0.0 reduce-scatter.5.cloned.1.call-update
  292.8 0.0 all-reduce.8.cloned.1.call-start
  292.9 81.5 %all-reduce.6.cloned.1.call-done = bf16[1024,1000]{1,0:T(8,128)(2,1)} async-done(((bf16[1024,1000]{1,0:T(8,128)(2,1)}), bf16[1024,1000]{1,0:T(8,128)(2,1)}) %all-reduce.6.cloned.1.call-update) | async-done | bytes 2048016 | tf_op jit(solution)/shard_map/psum | solution.py:73
  374.3 3.1 broadcast_select_fusion.1
  377.4 0.0 all-reduce.8.cloned.1.call-update
  377.5 0.0 copy-start.1
  377.5 4.9 %constant_dynamic-slice_fusion = f32[1024,1024]{1,0:T(8,128)} fusion(f32[1024,2048]{1,0:T(8,128)} %get-tuple-element.3, s32[]{:T(128)S(6)} %select_n.92), kind=kLoop, calls=%fused_computation.46 | loop fusion | bytes 8388612 | tf_op jit(solution)/shard_map/dynamic_slice | solution.py:71
  382.4 16.8 %gather_fusion = f32[1024]{0:T(1024)S(1)} fusion(f32[1024,1024]{1,0:T(8,128)} %constant_dynamic-slice_fusion, s32[1024]{0:T(1024)S(1)} %bitcast.30), kind=kCustom, calls=%fused_computation | custom fusion | bytes 16384 | tf_op jit(solution)/shard_map/jit(diagonal)/cond/branch_0_fun/gather | solution.py:72
  399.2 8.8 %psum.31 = bf16[1024]{0:T(1024)(128)(2,1)S(1)} all-reduce(bf16[1024]{0:T(1024)(128)(2,1)S(1)} %fusion.14), channel_id=1, replica_groups=mesh['trow'=4,'tcol'=4,'dp'=2] {'trow'}, use_global_device_ids=true, to_apply=%region_5.6 | all-reduce | flops 1024 | bytes 4096 | tf_op jit(solution)/shard_map/psum | solution.py:14
  407.9 0.0 reduce-scatter.5.cloned.1.call-done
  408.0 50.5 %all-reduce.8.cloned.1.call-done = bf16[1024,1000]{1,0:T(8,128)(2,1)} async-done(((bf16[1024,1000]{1,0:T(8,128)(2,1)}), bf16[1024,1000]{1,0:T(8,128)(2,1)}) %all-reduce.8.cloned.1.call-update) | async-done | bytes 2048016 | tf_op jit(solution)/shard_map/psum | solution.py:14
  458.4 2.7 divide_subtract_fusion
  461.2 0.0 copy-done.1
  (10 shorter events, 0.1 us)
Async XLA Ops:
  8.0 1.6 copy-start
  8.0 94.8 %all-gather.4.cloned.1.call-start = ((), (), s32[]{:S(2)}) async-start(), calls=%async_computation.2 | async-start | bytes 5242880 | tf_op jit(solution)/shard_map/all_gather | solution.py:32
  19.2 190.3 %all-reduce.4.cloned.1.call-start = ((), (), s32[]{:S(2)}) async-start(), calls=%async_computation.3 | async-start | bytes 8388608 | tf_op jit(solution)/shard_map/psum | solution.py:14
  107.3 132.7 %reduce-scatter.3.cloned.1.call-start = ((), (), s32[]{:S(2)}) async-start(), calls=%async_computation.4 | async-start | bytes 12582912 | tf_op jit(solution)/shard_map/reduce_scatter | solution.py:36
  223.5 1.2 copy-start.2
  223.5 39.4 %all-gather.6.cloned.1.call-start = ((), (), s32[]{:S(2)}) async-start(), calls=%async_computation.8 | async-start | bytes 4718592 | tf_op jit(solution)/shard_map/all_gather | solution.py:62
  225.6 148.8 %all-reduce.6.cloned.1.call-start = ((), (), s32[]{:S(2)}) async-start(), calls=%async_computation.5 | async-start | bytes 4194304 | tf_op jit(solution)/shard_map/psum | solution.py:73
  280.0 8.2 %copy-start.3 = (s32[1024]{0:T(1024)S(1)}, s32[1024]{0:T(1024)}, u32[]{:S(2)}) copy-start(s32[1024]{0:T(1024)} %param.8) | copy-start | bytes 12292
  288.1 119.9 %reduce-scatter.5.cloned.1.call-start = ((), (), s32[]{:S(2)}) async-start(), calls=%async_computation.7 | async-start | bytes 1572864 | tf_op jit(solution)/shard_map/reduce_scatter | solution.py:56
  292.8 165.6 %all-reduce.8.cloned.1.call-start = ((), (), s32[]{:S(2)}) async-start(), calls=%async_computation.6 | async-start | bytes 4194304 | tf_op jit(solution)/shard_map/psum | solution.py:14
  377.5 83.7 %copy-start.1 = (bf16[1024,1024]{1,0:T(8,128)(2,1)S(1)}, bf16[1024,1024]{1,0:T(8,128)(2,1)}, u32[]{:S(2)}) copy-start(bf16[1024,1024]{1,0:T(8,128)(2,1)} %param.5) | copy-start | bytes 6291460
Sparse Core Ops, SparseCore 0:
  19.3 83.4 all-gather.3
  107.4 101.9 all-reduce.3
  223.6 16.3 reduce-scatter.2
  288.2 86.1 all-reduce.5
  377.0 7.4 reduce-scatter.4
  387.4 70.9 all-reduce.7
Sparse Core Ops, SparseCore 1:
  226.4 36.4 all-gather.5
where the time goes:
time: 470 us; the launch traced here: 469 us
  waiting for transfers between devices  336 us (71%)
  matrix products  45.3 us (10%)
  local copies, waits for them, and re-layouts  45.2 us (10%)
  other arithmetic  16.9 us (4%)
  between operations  15.7 us (3%)
  blocking collectives  8.77 us (2%)
    psum x2, waiting for transfers between devices, broadcast(): return lax.psum(jnp.where(mine, array, jnp.zeros_like(array)), axis)  153 us
    all_gather x1, waiting for transfers between devices, shards(): left_feats = lax.all_gather(own_part, 'tcol', axis=1, tiled=True)  83.6 us
    psum x1, waiting for transfers between devices, shards(): lax.psum(curv_local.astype(jnp.bfloat16), 'tcol').astype(jnp.float32)  81.5 us
    gather x1, local copies, waits for them, and re-layouts, shards(): jnp.diagonal(diag_block) * (row_idx == col_idx).astype(jnp.float32)  16.8 us
    reduce_scatter x1, waiting for transfers between devices, shards(): lax.psum_scatter((lax.dot_general(left_feats, right_feats, contract, pref...  14.2 us
    dot_general x1, matrix products, shards(): lax.dot_general(left_feats, right_feats, contract, preferred_element_type...  14 us
    gather x5, local copies, waits for them, and re-layouts, shards(): chosen = jnp.take(gram_three, sub_index, axis=1)  12.8 us
    dot_general x1, matrix products, shards(): jnp.einsum('rpk,pkc->rpc', chosen, pieces, preferred_element_type=jnp.flo...  10.8 us
  transfers between devices with their start and end apart: 7, of which 6 were waited for; matrix products, arithmetic and copies ran while one was open for 10% of the time, Pallas kernels for 0%

commit v1 on v0

--- a/solution.py
+++ b/solution.py
@@ -11,7 +11,7 @@
 
 def broadcast(array, axis, root):
     mine = lax.axis_index(axis) == root
-    return lax.psum(jnp.where(mine, array, jnp.zeros_like(array)), axis)
+    return jnp.sum(lax.all_gather(jnp.where(mine, array, jnp.zeros_like(array)), axis), axis=0)
 
 
 def featurize(embeds, frequencies, phases):

time: 470 us -> 570 us (1.21)
  waiting for transfers between devices: 336 us -> 392 us
  other arithmetic: 16.9 us -> 41.5 us
  local copies, waits for them, and re-layouts: 45.2 us -> 69.1 us
    all_gather x0 -> x2, waiting for transfers between devices: none -> 205 us  [broadcast(): lax.all_gather(jnp.where(mine, array, jnp.zeros_like(array)), axis)]
    psum x2 -> x0, waiting for transfers between devices: 153 us -> none  [broadcast(): return lax.psum(jnp.where(mine, array, jnp.zeros_like(array)), axis)]
    reduce_sum x0 -> x3, other arithmetic: none -> 24.9 us  [broadcast(): jnp.sum(lax.all_gather(jnp.where(mine, array, jnp.zeros_like(array)), axi...]
    all_gather x0 -> x2, local copies, waits for them, and re-layouts: none -> 17.7 us  [broadcast(): lax.all_gather(jnp.where(mine, array, jnp.zeros_like(array)), axis)]
    psum x1 -> x0, blocking collectives: 8.77 us -> none  [broadcast(): return lax.psum(jnp.where(mine, array, jnp.zeros_like(array)), axis)]
    transpose x0 -> x1, local copies, waits for them, and re-layouts: none -> 6.82 us  [shards(): jnp.einsum('rpk,pkc->rpc', chosen, pieces, preferred_element_type=jnp.flo...]
    all_gather x0 -> x1, blocking collectives: none -> 6.79 us  [broadcast(): lax.all_gather(jnp.where(mine, array, jnp.zeros_like(array)), axis)]
  transfers between devices with their start and end apart: 7 -> 7, of which waited for: 6 -> 6; matrix products, arithmetic and copies ran while one was open for 10% -> 14% of each run, Pallas kernels for 0% -> 0%
where the time goes in v1:
time: 570 us; the launch traced here: 568 us
  waiting for transfers between devices  392 us (69%)
  local copies, waits for them, and re-layouts  69.1 us (12%)
  matrix products  42.2 us (7%)
  other arithmetic  41.5 us (7%)
  between operations  15.7 us (3%)
  blocking collectives  6.79 us (1%)
    all_gather x2, waiting for transfers between devices, broadcast(): lax.all_gather(jnp.where(mine, array, jnp.zeros_like(array)), axis)  205 us
    psum x1, waiting for transfers between devices, shards(): lax.psum(curv_local.astype(jnp.bfloat16), 'tcol').astype(jnp.float32)  84.9 us
    all_gather x1, waiting for transfers between devices, shards(): left_feats = lax.all_gather(own_part, 'tcol', axis=1, tiled=True)  83.6 us
    reduce_sum x3, other arithmetic, broadcast(): jnp.sum(lax.all_gather(jnp.where(mine, array, jnp.zeros_like(array)), axi...  24.9 us
    all_gather x2, local copies, waits for them, and re-layouts, broadcast(): lax.all_gather(jnp.where(mine, array, jnp.zeros_like(array)), axis)  17.7 us
    gather x1, local copies, waits for them, and re-layouts, shards(): jnp.diagonal(diag_block) * (row_idx == col_idx).astype(jnp.float32)  17.3 us
    reduce_scatter x1, waiting for transfers between devices, shards(): lax.psum_scatter((lax.dot_general(left_feats, right_feats, contract, pref...  14.2 us
    dot_general x1, matrix products, shards(): lax.dot_general(left_feats, right_feats, contract, preferred_element_type...  14 us
  transfers between devices with their start and end apart: 7, of which 6 were waited for; matrix products, arithmetic and copies ran while one was open for 14% of the time, Pallas kernels for 0%

profile of v1, /device:TPU:0, one launch (start us, length us, event | category | flops | bytes accessed | tf_op | source)
XLA Modules:
  0.0 568.0 jit_solution(1629967506376602687)
XLA Ops:
  8.0 0.0 copy-start
  8.0 0.0 all-gather.9.cloned.1.call-start
  8.1 1.5 copy-done
  9.6 9.6 %multiply_convert_fusion.1 = bf16[1024,512]{1,0:T(8,128)(2,1)} fusion(bf16[1024,1024]{1,0:T(8,128)(2,1)S(1)} %copy-done, bf16[1024,512]{1,0:T(8,128)(2,1)} %param.6, f32[512]{0:T(512)} %param.7), kind=kOutput, calls=%fused_computation.17 | convolution fusion | flops 1075314688 | bytes 4196352 | tf_op jit(solution)/shard_map/dot_general | solution.py:18
  19.2 0.0 all-gather.9.cloned.1.call-update
  19.2 0.0 all-gather.11.cloned.1.call-start
  19.3 83.6 %all-gather.9.cloned.1.call-done = bf16[1024,2048]{1,0:T(8,128)(2,1)} async-done(((bf16[1024,512]{1,0:T(8,128)(2,1)}), bf16[1024,2048]{1,0:T(8,128)(2,1)}) %all-gather.9.cloned.1.call-update) | async-done | bytes 4194320 | tf_op jit(solution)/shard_map/all_gather | solution.py:32
  102.8 4.5 broadcast_select_fusion
  107.3 0.0 all-gather.11.cloned.1.call-update
  107.3 0.0 reduce-scatter.3.cloned.1.call-start
  107.4 155.8 %all-gather.11.cloned.1.call-done = bf16[4096,2048]{1,0:T(8,128)(2,1)} async-done(((bf16[1024,2048]{1,0:T(8,128)(2,1)}), bf16[4096,2048]{1,0:T(8,128)(2,1)}) %all-gather.11.cloned.1.call-update) | async-done | bytes 16777232 | tf_op jit(solution)/shard_map/all_gather | solution.py:14
  263.1 12.0 %reduce_sum.36 = bf16[1024,2048]{1,0:T(8,128)(2,1)} reduce(bf16[4,1024,2048]{2,1,0:T(8,128)(2,1)} %bitcast.36, bf16[]{:T(256)} %constant.76.clone.1), dimensions={0}, to_apply=%region_0.1 | reduce | flops 6291456 | bytes 20971522 | tf_op jit(solution)/shard_map/reduce_sum | solution.py:14
  275.2 14.0 %multiply_convert_fusion = bf16[2048,2048]{1,0:T(8,128)(2,1)} fusion(bf16[1024,2048]{1,0:T(8,128)(2,1)} %all-gather.9.cloned.1.call-done, bf16[1024,2048]{1,0:T(8,128)(2,1)} %reduce_sum.36), kind=kOutput, calls=%fused_computation.7 | convolution fusion | flops 8598323200 | bytes 16777216 | tf_op jit(solution)/shard_map/dot_general | solution.py:38
  289.2 0.0 copy-start.2
  289.2 0.0 reduce-scatter.3.cloned.1.call-update
  289.2 0.0 all-gather.13.cloned.1.call-start
  289.3 1.1 copy-done.2
  290.4 0.8 convert_element_type.69
  291.3 0.0 all-gather.13.cloned.1.call-update
  291.3 0.2 all-reduce.2.cloned.1.call-start
  291.6 14.2 %reduce-scatter.3.cloned.1.call-done = bf16[1024,2048]{1,0:T(8,128)(2,1)} async-done(((bf16[2048,2048]{1,0:T(8,128)(2,1)}), bf16[1024,2048]{1,0:T(8,128)(2,1)}) %reduce-scatter.3.cloned.1.call-update) | async-done | bytes 4194320 | tf_op jit(solution)/shard_map/reduce_scatter | solution.py:36
  305.8 5.8 %fusion.17 = (bf16[1024,2048]{1,0:T(8,128)(2,1)S(1)}, f32[1024,2048]{1,0:T(8,128)}) fusion(s32[2048]{0:T(1024)S(1)} %iota_add_fusion, s32[1024]{0:T(1024)S(1)} %iota_add_fusion.1, bf16[1024,2048]{1,0:T(8,128)(2,1)} %reduce-scatter.3.cloned.1.call-done), kind=kLoop, calls=%fused_computation.47 | loop fusion | flops 10485760 | bytes 16789504 | tf_op jit(solution)/shard_map/convert_element_type | solution.py:59
  311.5 0.6 fusion.18
  312.1 0.2 copy.32
  312.3 1.6 copy.33
  313.9 4.4 gather_fusion.2
  318.3 6.1 %gather_fusion.1 = bf16[8,512,1024]{2,1,0:T(8,128)(2,1)} fusion(bf16[512,2,1024]{2,0,1:T(8,128)(2,1)} %bitcast.35, s32[1024]{0:T(1024)S(1)} %pad_clamp_fusion), kind=kCustom, calls=%fused_computation.1 | custom fusion | bytes 16777248 | tf_op jit(solution)/shard_map/jit(_take)/gather | solution.py:66
  324.3 4.3 all-gather.13.cloned.1.call-done
  328.7 10.8 %fusion.5 = bf16[1024,8,250]{2,0,1:T(8,128)(2,1)} fusion(bf16[8,1024,250]{2,1,0:T(8,128)(2,1)} %bitcast.41, bf16[512,8,1024]{2,0,1:T(8,128)(2,1)} %bitcast.37, bf16[512,8,1024]{2,0,1:T(8,128)(2,1)} %bitcast.38, pred[8]{0:T(512)(128)(4,1)S(1)} %compare_and_fusion), kind=kOutput, calls=%fused_computation.12 | convolution fusion | flops 4236247040 | bytes 24969224 | tf_op jit(solution)/shard_map/rpk,pkc->rpc/dot_general | solution.py:67
  339.4 6.8 %copy.22 = bf16[1024,8,250]{0,1,2:T(8,128)(2,1)} copy(bf16[1024,8,250]{2,0,1:T(8,128)(2,1)} %fusion.5) | data formatting | bytes 8192000 | tf_op jit(solution)/shard_map/rpk,pkc->rpc/transpose | solution.py:67
  346.2 3.4 convert_bitcast_fusion
  349.6 0.6 copy.23
  350.2 1.9 convert_element_type.72
  352.1 0.0 copy-start.4
  352.1 0.0 all-reduce.2.cloned.1.call-update
  352.1 0.0 all-gather.15.cloned.1.call-start
  352.2 84.9 %all-reduce.2.cloned.1.call-done = bf16[1024,1000]{0,1:T(8,128)(2,1)} async-done(((bf16[1024,1000]{0,1:T(8,128)(2,1)}), bf16[1024,1000]{0,1:T(8,128)(2,1)}) %all-reduce.2.cloned.1.call-update) | async-done | bytes 2048016 | tf_op jit(solution)/shard_map/psum | solution.py:73
  437.1 3.1 broadcast_select_fusion.1
  440.2 0.0 all-gather.15.cloned.1.call-update
  440.2 0.0 reduce-scatter.5.cloned.1.call-start
  440.3 0.0 copy-done.4
  440.3 4.5 fusion.6
  444.8 0.0 reduce-scatter.5.cloned.1.call-update
  444.8 1.3 copy.25
  446.1 5.5 constant_dynamic-slice_fusion
  451.7 17.3 %gather_fusion = f32[1024]{0:T(1024)S(1)} fusion(f32[1024,1024]{1,0:T(8,128)} %constant_dynamic-slice_fusion, s32[1024]{0:T(1024)S(1)} %bitcast.33), kind=kCustom, calls=%fused_computation | custom fusion | bytes 16384 | tf_op jit(solution)/shard_map/jit(diagonal)/cond/branch_0_fun/gather | solution.py:72
  468.9 6.8 %all-gather.3 = bf16[4096]{0:T(1024)(128)(2,1)S(1)} all-gather(bf16[1024]{0:T(1024)(128)(2,1)S(1)} %fusion.10), channel_id=5, replica_groups=mesh['trow'=4,'tcol'=4,'dp'=2] {'trow'}, dimensions={0}, use_global_device_ids=true | all-gather | bytes 10240 | tf_op jit(solution)/shard_map/all_gather | solution.py:14
  475.8 49.3 %all-gather.15.cloned.1.call-done = bf16[4096,1000]{0,1:T(8,128)(2,1)} async-done(((bf16[1024,1000]{0,1:T(8,128)(2,1)}), bf16[4096,1000]{0,1:T(8,128)(2,1)}) %all-gather.15.cloned.1.call-update) | async-done | bytes 8192016 | tf_op jit(solution)/shard_map/all_gather | solution.py:14
  525.0 17.7 %reshape.121 = bf16[4,1024,1000]{1,0,2:T(4,128)(2,1)} reshape(bf16[4096,1000]{0,1:T(8,128)(2,1)} %all-gather.15.cloned.1.call-done) | data formatting | bytes 16384000 | tf_op jit(solution)/shard_map/all_gather | solution.py:14
  542.7 0.0 copy-start.3
  542.7 0.0 copy-start.1
  542.7 12.8 %reduce_sum.37 = bf16[1024,1000]{0,1:T(8,128)(2,1)} reduce(bf16[4,1024,1000]{1,0,2:T(4,128)(2,1)} %reshape.121, bf16[]{:T(256)} %constant.76.clone.1), dimensions={0}, to_apply=%region_3.4 | reduce | flops 3072000 | bytes 10240002 | tf_op jit(solution)/shard_map/reduce_sum | solution.py:14
  555.5 0.0 reduce-scatter.5.cloned.1.call-done
  555.5 0.0 copy-done.3
  555.5 2.5 divide_subtract_fusion
  558.0 2.5 copy.26
  560.5 0.0 copy-done.1
  (12 shorter events, 0.1 us)
Async XLA Ops:
  8.0 1.6 copy-start
  8.0 94.8 %all-gather.9.cloned.1.call-start = ((), (), s32[]{:S(2)}) async-start(), calls=%async_computation.2 | async-start | bytes 5242880 | tf_op jit(solution)/shard_map/all_gather | solution.py:32
  19.2 243.9 %all-gather.11.cloned.1.call-start = ((), (), s32[]{:S(2)}) async-start(), calls=%async_computation.6 | async-start | bytes 20971520 | tf_op jit(solution)/shard_map/all_gather | solution.py:14
  107.3 198.4 %reduce-scatter.3.cloned.1.call-start = ((), (), s32[]{:S(2)}) async-start(), calls=%async_computation.3 | async-start | bytes 12582912 | tf_op jit(solution)/shard_map/reduce_scatter | solution.py:36
  289.2 1.2 copy-start.2
  289.2 39.4 %all-gather.13.cloned.1.call-start = ((), (), s32[]{:S(2)}) async-start(), calls=%async_computation.7 | async-start | bytes 4718592 | tf_op jit(solution)/shard_map/all_gather | solution.py:62
  291.3 145.8 %all-reduce.2.cloned.1.call-start = ((), (), s32[]{:S(2)}) async-start(), calls=%async_computation.4 | async-start | bytes 4096000 | tf_op jit(solution)/shard_map/psum | solution.py:73
  352.1 88.2 %copy-start.4 = (s32[1024]{0:T(1024)S(1)}, s32[1024]{0:T(1024)}, u32[]{:S(2)}) copy-start(s32[1024]{0:T(1024)} %param.8) | copy-start | bytes 12292
  352.1 172.9 %all-gather.15.cloned.1.call-start = ((), (), s32[]{:S(2)}) async-start(), calls=%async_computation.8 | async-start | bytes 10240000 | tf_op jit(solution)/shard_map/all_gather | solution.py:14
  440.2 115.3 %reduce-scatter.5.cloned.1.call-start = ((), (), s32[]{:S(2)}) async-start(), calls=%async_computation.5 | async-start | bytes 1572864 | tf_op jit(solution)/shard_map/reduce_scatter | solution.py:56
  542.7 12.8 %copy-start.3 = (f32[1024,250]{0,1:T(8,128)S(1)}, f32[1024,250]{0,1:T(8,128)}, u32[]{:S(2)}) copy-start(f32[1024,250]{0,1:T(8,128)} %copy.25) | copy-start | bytes 3072004
  542.7 17.8 %copy-start.1 = (bf16[1024,1024]{1,0:T(8,128)(2,1)S(1)}, bf16[1024,1024]{1,0:T(8,128)(2,1)}, u32[]{:S(2)}) copy-start(bf16[1024,1024]{1,0:T(8,128)(2,1)} %param.5) | copy-start | bytes 6291460
Sparse Core Ops, SparseCore 0:
  19.3 83.4 all-gather.8
  107.4 155.6 all-gather.10
  289.3 16.3 reduce-scatter.2
  352.3 84.8 all-reduce.1
  440.3 84.6 all-gather.14
  527.1 8.3 reduce-scatter.4
Sparse Core Ops, SparseCore 1:
  292.2 36.4 all-gather.12
